TPU v7x, 256 devices: a whole 4x4x8 slice. The times are simulated.
256 devices in a mesh: pop: 64 (over x, z, core), mp: 4 (over y).
Axes of the slice: x: 4, y: 4, z: 8, core: 2. Of those that a mesh axis runs over, the one named last changes fastest.
Arguments:
- tokens: bfloat16 [256, 3584], replicated, may hold values from -60 to 60
- target: bfloat16 [256, 3584], P(None, 'mp'), may hold values from -6 to 6
- w_query: bfloat16 [3584, 3584], P('pop', 'mp'), may hold values from -0.09375 to 0.09375
- w_key: bfloat16 [3584, 512], P(None, 'mp'), may hold values from -0.09375 to 0.09375
- w_value: bfloat16 [3584, 512], P(None, 'mp'), may hold values from -0.09375 to 0.09375
- w_out: bfloat16 [3584, 3584], P('mp', 'pop'), may hold values from -0.09375 to 0.09375
- query_left_factors: bfloat16 [64, 3584, 4], P('pop'), may hold values from -0.09375 to 0.09375
- query_right_factors: bfloat16 [64, 4, 3584], P('pop', None, 'mp'), may hold values from -6 to 6
- o_left: bfloat16 [64, 3584, 4], P('pop', 'mp'), may hold values from -0.09375 to 0.09375
- o_right: bfloat16 [64, 4, 3584], P('pop'), may hold values from -6 to 6
- member_ids: int32 [64], P('pop'), may hold values from 0 to 63, each once
Outputs:
- grad_query: float32 [3584, 3584], P('pop', 'mp')
- grad_out: float32 [3584, 3584], P('mp', 'pop')
- fitness: float32 [64], P('pop')
Inputs may be any that keep to these rules, and one draw needn't show every extreme that they name: `member_ids`: every number from 0 to 63 appears once.
All inputs are finite; a program needn't handle non-finite values.
Results may differ from a plain program's by a relative error of at most 0.005.
Values may be sent and summed in bfloat16 or wider, within the bound.
No kernel may reach another device: no remote copies, remote signals or barrier semaphores. Data moves between devices by JAX's collectives and lax.ppermute only.
A program may use at most 64 MiB of HBM per device.

v0:
```python
import math
import jax
import jax.numpy as jnp
from jax import lax
from jax.sharding import Mesh
from jax.sharding import PartitionSpec as P

D = 3584
HEADS = 28
KV_HEADS = 4
HEAD_DIM = 128
RANK = 4
POP = ("pop_0", "pop_1", "pop_2")
noise_scale = 0.5
rope_base = 1000000.0
spread_floor = 0.001


def in_order(parts, dim):
    parts = jnp.moveaxis(parts, 0, dim)
    shape = parts.shape
    return parts.reshape(*shape[:dim], shape[dim] * shape[dim + 1], *shape[dim + 2 :])


def all_blocks(shard, axes, turns):
    parts = shard[None]
    for k in turns:
        parts = lax.all_gather(parts, axes[k], axis=0, tiled=True)
    held = [lax.axis_size(axes[k]) for k in reversed(turns)]
    parts = parts.reshape(*held, *shard.shape)
    turned = sorted(range(len(turns)), key=lambda place: turns[len(turns) - 1 - place])
    return parts.transpose(*turned, *range(len(turns), parts.ndim)).reshape(-1, *shard.shape)


def whole_of(shard, axes, turns, dim):
    return in_order(all_blocks(shard, axes, turns), dim)


def cut_along(shard, dim, devices):
    before, after = (shard.shape[:dim], shard.shape[dim + 1 :])
    return jnp.moveaxis(shard.reshape(*before, devices, -1, *after), dim, 0)


def summed_on_arrival(shard, axis, dim):
    devices = lax.axis_size(axis)
    parts = lax.all_to_all(cut_along(shard, dim, devices), axis, 0, 0, tiled=True)
    return jnp.sum(parts.astype(jnp.float32), axis=0)


def copy_for_each(shard, axis):
    copies = jnp.broadcast_to(shard, (lax.axis_size(axis), *shard.shape))
    return lax.all_to_all(copies, axis, split_axis=0, concat_axis=0, tiled=True)


def of_everyone(shard, axis):
    return copy_for_each(shard, axis).sum(axis=0)


def gathered_copies(shard, axis, dim):
    return in_order(copy_for_each(shard, axis), dim)


def side_by_side(arrays, axis, dim, along):
    columns = [a.reshape(*a.shape[:along], -1) for a in arrays]
    both = jnp.concatenate(columns, axis=along)
    result, at, done = (lax.all_gather(both, axis, axis=dim, tiled=True), 0, [])
    for a, column in zip(arrays, columns):
        share = result[..., at : at + column.shape[along]]
        done.append(share.reshape(*share.shape[:along], *a.shape[along:]))
        at += column.shape[along]
    return tuple(done)


def tables(count, head_size):
    position = jnp.arange(count, dtype=jnp.float32)
    index = jnp.arange(head_size // 2, dtype=jnp.float32)
    freq = jnp.exp(-math.log(rope_base) * 2.0 * index / head_size)
    angle = position[:, None] * freq[None, :]
    return (jnp.cos(angle)[:, None, :], jnp.sin(angle)[:, None, :])


def rotate(field, cosine_table, sine):
    half = field.shape[-1] // 2
    first = field[..., :half]
    second = field[..., half:]
    return jnp.concatenate(
        [first * cosine_table - second * sine, second * cosine_table + first * sine], axis=-1
    )


def per_device(
    tokens,
    target,
    w_query,
    w_key,
    w_value,
    w_out,
    query_left_factors,
    query_right_factors,
    o_left,
    o_right,
    member_ids,
):
    tok = tokens.shape[0]
    local_feats = w_query.shape[1]
    local_kv = w_key.shape[1] // HEAD_DIM
    group = HEADS // KV_HEADS
    local_heads = local_kv * group
    slots = query_left_factors.shape[0]
    scale = HEAD_DIM ** (-0.5)
    cosine_table, sine = tables(tok, HEAD_DIM)
    base = jnp.dot(tokens, whole_of(w_query, POP, (0, 1, 2), 0), preferred_element_type=jnp.float32)
    keys = rotate(
        jnp.dot(tokens, w_key, preferred_element_type=jnp.float32).reshape(tok, local_kv, HEAD_DIM),
        cosine_table,
        sine,
    ).astype(jnp.bfloat16)
    values = (
        jnp.dot(tokens, w_value, preferred_element_type=jnp.float32)
        .astype(jnp.bfloat16)
        .reshape(tok, local_kv, HEAD_DIM)
    )
    signs = (1 - 2 * (member_ids % 2)).astype(jnp.float32)
    factor = noise_scale * signs[:, None, None]
    lowrank_product = jnp.einsum(
        "td,mdr->mtr", tokens, query_left_factors, preferred_element_type=jnp.float32
    ).astype(jnp.bfloat16)
    query = base[None] + factor * jnp.einsum(
        "olj,ojv->olv", lowrank_product, query_right_factors, preferred_element_type=jnp.float32
    )
    query = rotate(
        query.reshape(slots, tok, local_heads, HEAD_DIM), cosine_table[None], sine[None]
    ).astype(jnp.bfloat16)
    query = query.reshape(slots, tok, local_kv, group, HEAD_DIM)
    scores = jnp.einsum("mtkgd,skd->mkgts", query, keys, preferred_element_type=jnp.float32) * scale
    causal = jnp.arange(tok)[:, None] >= jnp.arange(tok)[None, :]
    scores = jnp.where(causal, scores, -1e30)
    probs = jax.nn.softmax(scores, axis=-1).astype(jnp.bfloat16)
    mixed = (
        jnp.einsum("mkgts,skd->mtkgd", probs, values, preferred_element_type=jnp.float32)
        .astype(jnp.bfloat16)
        .reshape(slots, tok, local_feats)
    )
    low_out = jnp.einsum("mtf,mfr->mtr", mixed, o_left, preferred_element_type=jnp.float32)
    right_full = o_right.astype(jnp.float32)
    part = jnp.einsum(
        "mtf,fe->mte",
        mixed,
        lax.all_gather(w_out, POP, axis=1, tiled=True),
        preferred_element_type=jnp.float32,
    )
    term = part + factor * jnp.einsum(
        "mtr,mre->mte", low_out, right_full, precision=lax.Precision.HIGHEST
    )
    output = summed_on_arrival(term.astype(jnp.bfloat16), "mp", 2)
    diff = output - target.astype(jnp.float32)[None]
    errors = of_everyone(jnp.sum(diff * diff, axis=(1, 2)), "mp")
    fitness = -(errors / (tok * D))
    count = slots * lax.axis_size(POP)
    everyone = gathered_copies(fitness, POP, 0)
    mean = jnp.sum(everyone) / count
    spread = jnp.sum((everyone - mean) * (everyone - mean)) / count
    weight = signs * (fitness - mean) / jnp.sqrt(spread + spread_floor)
    every_weight = gathered_copies(weight, POP, 0)
    right_factors_gathered, left_all = side_by_side((query_right_factors, o_left), POP, 0, 1)
    rows_q = lax.all_to_all(query_left_factors, POP, split_axis=1, concat_axis=0, tiled=True)
    cols_o = lax.all_to_all(o_right, POP, split_axis=2, concat_axis=0, tiled=True)
    whole_population = rows_q.shape[0]
    left_q = jnp.transpose(
        rows_q.astype(jnp.float32) * every_weight[:, None, None], (1, 0, 2)
    ).reshape(rows_q.shape[1], whole_population * RANK)
    right_q = right_factors_gathered.astype(jnp.float32).reshape(
        whole_population * RANK, local_feats
    )
    grad_query = jnp.dot(left_q, right_q, precision=lax.Precision.HIGHEST) / noise_scale
    output_left_factor = jnp.transpose(
        left_all.astype(jnp.float32) * every_weight[:, None, None], (1, 0, 2)
    ).reshape(local_feats, whole_population * RANK)
    right_o = cols_o.astype(jnp.float32).reshape(whole_population * RANK, cols_o.shape[2])
    grad_out = jnp.dot(output_left_factor, right_o, precision=lax.Precision.HIGHEST) / noise_scale
    return (grad_query, grad_out, fitness)


def solution(mesh):
    torus = Mesh(mesh.devices.reshape(4, 8, 2, mesh.shape["mp"]), ("pop_0", "pop_1", "pop_2", "mp"))
    placed = (
        P(),
        P(None, "mp"),
        P(POP, "mp"),
        P(None, "mp"),
        P(None, "mp"),
        P("mp", POP),
        P(POP, None, None),
        P(POP, None, "mp"),
        P(POP, "mp", None),
        P(POP, None, None),
        P(POP),
    )
    return jax.shard_map(
        per_device,
        mesh=torus,
        in_specs=placed,
        out_specs=(P(POP, "mp"), P("mp", POP), P(POP)),
        check_vma=False,
    )
```

profile of v0, /device:TPU:1, one launch (start us, length us, event | category | flops | bytes accessed | tf_op | source)
XLA Modules:
  0.0 428.7 jit_solution(7784847421207332163)
XLA Ops:
  7.2 13.0 %all-gather = bf16[224,896]{1,0:T(8,128)(2,1)} all-gather(bf16[56,896]{1,0:T(8,128)(2,1)} %param.13), channel_id=2, replica_groups=mesh['pop_0'=4,'pop_1'=8,'pop_2'=2,'mp'=4] {'pop_0'}, dimensions={0}, use_global_device_ids=true | all-gather | bytes 501760 | tf_op jit(solution)/shard_map/all_gather | solution.py:28
  20.3 49.6 %all-gather.6.cloned.1.call-done = bf16[32,56,896]{2,1,0:T(8,128)(2,1)} async-done(((bf16[4,56,896]{2,1,0:T(8,128)(2,1)}), bf16[32,56,896]{2,1,0:T(8,128)(2,1)}) %all-gather.6.cloned.1.call-update) | async-done | bytes 3211280 | tf_op jit(solution)/shard_map/all_gather | solution.py:28
  73.6 19.9 %all-gather.8.cloned.1.call-done = bf16[64,56,896]{2,1,0:T(8,128)(2,1)} async-done(((bf16[32,56,896]{2,1,0:T(8,128)(2,1)}), bf16[64,56,896]{2,1,0:T(8,128)(2,1)}) %all-gather.8.cloned.1.call-update) | async-done | bytes 6422544 | tf_op jit(solution)/shard_map/all_gather | solution.py:28
  93.5 3.3 copy.114
  96.9 2.1 fusion.29
  99.1 2.1 fusion.3
  101.1 1.5 copy.115
  110.0 2.6 convolution_convert_fusion
  112.8 65.1 %all-gather.10.cloned.1.call-done = bf16[896,3584]{0,1:T(8,128)(2,1)} async-done(((bf16[896,56]{0,1:T(8,128)(2,1)}), bf16[896,3584]{0,1:T(8,128)(2,1)}) %all-gather.10.cloned.1.call-update) | async-done | bytes 6422544 | tf_op jit(solution)/shard_map/all_gather | solution.py:149
  177.9 4.9 %fusion.30 = f32[256,3584]{1,0:T(8,128)S(1)} fusion(bf16[256,896]{0,1:T(8,128)(2,1)S(1)} %bitcast.106, bf16[896,3584]{0,1:T(8,128)(2,1)} %all-gather.10.cloned.1.call-done), kind=kOutput, calls=%fused_computation.58 | convolution fusion | flops 1644167168 | bytes 10551296 | tf_op jit(solution)/shard_map/mtf,fe->mte/dot_general | solution.py:146
  182.8 3.1 fusion.1
  185.9 3.3 reshape.288
  189.2 1.5 copy.145
  190.7 4.0 all-to-all-start.1
  195.3 22.5 %all-to-all-done.1 = bf16[4,1,256,896]{3,2,1,0:T(8,128)(2,1)S(1)} async-done(((bf16[4,1,256,896]{3,2,1,0:T(8,128)(2,1)}), bf16[4,1,256,896]{3,2,1,0:T(8,128)(2,1)S(1)}, u32[]{:S(2)}, u32[]{:S(2)}) %all-to-all-start.1) | async-done | bytes 1835040 | tf_op jit(solution)/shard_map/all_to_all | solution.py:46
  219.6 6.5 %all_to_all.47 = f32[4,1,1]{2,1,0:T(1,128)S(1)} all-to-all(f32[4,1,1]{2,1,0:T(1,128)S(1)} %broadcast_in_dim.34), channel_id=1, replica_groups=mesh['pop_0'=4,'pop_1'=8,'pop_2'=2,'mp'=4] {'mp'}, dimensions={0} | all-to-all | bytes 32 | tf_op jit(solution)/shard_map/all_to_all | solution.py:52
  227.9 7.9 %all-to-all-start.3 = ((f32[64,1,1]{2,1,0:T(1,128)}), f32[64,1,1]{2,1,0:T(1,128)S(1)}, u32[]{:S(2)}, u32[]{:S(2)}) async-start(f32[64,1,1]{2,1,0:T(1,128)} %broadcast_in_dim.35), calls=%async_computation.3 | async-start | bytes 65536 | tf_op jit(solution)/shard_map/all_to_all | solution.py:52
  235.9 51.8 %all-gather.1 = bf16[64,1,7168]{2,1,0:T(2,128)(2,1)S(1)} all-gather(bf16[1,1,7168]{2,1,0:T(2,128)(2,1)S(1)} %maximum_bitcast_fusion.2), channel_id=1, replica_groups=mesh['pop_0'=4,'pop_1'=8,'pop_2'=2,'mp'=4] {'pop_0','pop_1','pop_2'}, dimensions={0}, use_global_device_ids=true | all-gather | bytes 931840 | tf_op jit(solution)/shard_map/all_gather | solution.py:66
  287.7 3.2 copy.129
  292.2 7.3 %all-to-all-start.5 = ((bf16[1,4,3584]{1,0,2:T(2,128)(2,1)}), bf16[1,4,3584]{1,0,2:T(2,128)(2,1)S(1)}, u32[]{:S(2)}, u32[]{:S(2)}) async-start(bf16[1,4,3584]{1,0,2:T(2,128)(2,1)} %copy.129), calls=%async_computation.5 | async-start | bytes 3670016 | tf_op jit(solution)/shard_map/all_to_all | solution.py:167
  299.4 2.0 slice_convert_fusion
  301.5 3.2 copy.112
  306.1 38.7 %all-to-all-done.5 = bf16[1,4,3584]{1,0,2:T(2,128)(2,1)S(1)} async-done(((bf16[1,4,3584]{1,0,2:T(2,128)(2,1)}), bf16[1,4,3584]{1,0,2:T(2,128)(2,1)S(1)}, u32[]{:S(2)}, u32[]{:S(2)}) %all-to-all-start.5) | async-done | bytes 28704 | tf_op jit(solution)/shard_map/all_to_all | solution.py:167
  344.8 6.2 %all-to-all-start = ((bf16[1,3584,4]{2,0,1:T(2,128)(2,1)}), bf16[1,3584,4]{2,0,1:T(2,128)(2,1)}, u32[]{:S(2)}, u32[]{:S(2)}) async-start(bf16[1,3584,4]{2,0,1:T(2,128)(2,1)} %copy.112), calls=%async_computation | async-start | bytes 3670016 | tf_op jit(solution)/shard_map/all_to_all | solution.py:166
  352.3 44.0 %all-to-all-done = bf16[1,3584,4]{2,0,1:T(2,128)(2,1)} async-done(((bf16[1,3584,4]{2,0,1:T(2,128)(2,1)}), bf16[1,3584,4]{2,0,1:T(2,128)(2,1)}, u32[]{:S(2)}, u32[]{:S(2)}) %all-to-all-start) | async-done | bytes 28704 | tf_op jit(solution)/shard_map/all_to_all | solution.py:166
  396.9 6.0 %all-to-all-start.4 = ((f32[64,1,1]{2,1,0:T(1,128)}), f32[64,1,1]{2,1,0:T(1,128)S(1)}, u32[]{:S(2)}, u32[]{:S(2)}) async-start(f32[64,1,1]{2,1,0:T(1,128)} %broadcast_in_dim.36), calls=%async_computation.4 | async-start | bytes 65536 | tf_op jit(solution)/shard_map/all_to_all | solution.py:52
  403.0 1.8 copy.127
  406.0 1.8 copy.130
  408.1 3.7 copy.113
  412.8 1.6 multiply_bitcast_fusion
  414.4 2.8 copy.128
  417.2 1.5 reshape.293
  (71 shorter events, 22.1 us)
Async XLA Ops:
  7.2 64.2 %copy-start = (bf16[256,3584]{1,0:T(8,128)(2,1)S(1)}, bf16[256,3584]{1,0:T(8,128)(2,1)}, u32[]{:S(2)}) copy-start(bf16[256,3584]{1,0:T(8,128)(2,1)} %param.11) | copy-start | bytes 5505028
  7.2 62.7 %all-gather.6.cloned.1.call-start = ((), (), s32[]{:S(2)}) async-start(), calls=%async_computation.6 | async-start | bytes 3612672 | tf_op jit(solution)/shard_map/all_gather | solution.py:28
  20.2 51.2 %copy-start.4 = (bf16[3584,128]{1,0:T(8,128)(2,1)S(1)}, bf16[3584,128]{1,0:T(8,128)(2,1)}, u32[]{:S(2)}) copy-start(bf16[3584,128]{1,0:T(8,128)(2,1)} %param.14) | copy-start | bytes 2752516
  20.3 73.3 %all-gather.8.cloned.1.call-start = ((), (), s32[]{:S(2)}) async-start(), calls=%async_computation.7 | async-start | bytes 9633792 | tf_op jit(solution)/shard_map/all_gather | solution.py:28
  69.9 107.9 %all-gather.10.cloned.1.call-start = ((), (), s32[]{:S(2)}) async-start(), calls=%async_computation.8 | async-start | bytes 6522880 | tf_op jit(solution)/shard_map/all_gather | solution.py:149
  96.9 2.2 copy-start.9
  96.9 2.2 copy-start.11
  106.1 1.4 copy-start.6
  106.1 1.4 copy-start.7
  108.1 1.3 copy-start.2
  108.2 1.9 copy-start.13
  110.0 2.6 copy-start.12
  112.8 70.0 %copy-start.8 = (bf16[1,4,3584]{2,1,0:T(4,128)(2,1)S(1)}, bf16[1,4,3584]{2,1,0:T(4,128)(2,1)}, u32[]{:S(2)}) copy-start(bf16[1,4,3584]{2,1,0:T(4,128)(2,1)} %param.20) | copy-start | bytes 86020
  190.7 27.1 %all-to-all-start.1 = ((bf16[4,1,256,896]{3,2,1,0:T(8,128)(2,1)}), bf16[4,1,256,896]{3,2,1,0:T(8,128)(2,1)S(1)}, u32[]{:S(2)}, u32[]{:S(2)}) async-start(bf16[4,1,256,896]{3,2,1,0:T(8,128)(2,1)} %bitcast.98), calls=%async_computation.1 | async-start | bytes 3670016 | tf_op jit(solution)/shard_map/all_to_all | solution.py:46
  194.7 23.3 %copy-start.5 = (bf16[256,896]{1,0:T(8,128)(2,1)S(1)}, bf16[256,896]{1,0:T(8,128)(2,1)}, u32[]{:S(2)}) copy-start(bf16[256,896]{1,0:T(8,128)(2,1)} %param.12) | copy-start | bytes 1376260
  227.9 64.2 %all-to-all-start.3 = ((f32[64,1,1]{2,1,0:T(1,128)}), f32[64,1,1]{2,1,0:T(1,128)S(1)}, u32[]{:S(2)}, u32[]{:S(2)}) async-start(f32[64,1,1]{2,1,0:T(1,128)} %broadcast_in_dim.35), calls=%async_computation.3 | async-start | bytes 65536 | tf_op jit(solution)/shard_map/all_to_all | solution.py:52
  292.2 52.6 %all-to-all-start.5 = ((bf16[1,4,3584]{1,0,2:T(2,128)(2,1)}), bf16[1,4,3584]{1,0,2:T(2,128)(2,1)S(1)}, u32[]{:S(2)}, u32[]{:S(2)}) async-start(bf16[1,4,3584]{1,0,2:T(2,128)(2,1)} %copy.129), calls=%async_computation.5 | async-start | bytes 3670016 | tf_op jit(solution)/shard_map/all_to_all | solution.py:167
  299.4 2.1 copy-start.10
  344.8 51.5 %all-to-all-start = ((bf16[1,3584,4]{2,0,1:T(2,128)(2,1)}), bf16[1,3584,4]{2,0,1:T(2,128)(2,1)}, u32[]{:S(2)}, u32[]{:S(2)}) async-start(bf16[1,3584,4]{2,0,1:T(2,128)(2,1)} %copy.112), calls=%async_computation | async-start | bytes 3670016 | tf_op jit(solution)/shard_map/all_to_all | solution.py:166
  396.9 15.3 %all-to-all-start.4 = ((f32[64,1,1]{2,1,0:T(1,128)}), f32[64,1,1]{2,1,0:T(1,128)S(1)}, u32[]{:S(2)}, u32[]{:S(2)}) async-start(f32[64,1,1]{2,1,0:T(1,128)} %broadcast_in_dim.36), calls=%async_computation.4 | async-start | bytes 65536 | tf_op jit(solution)/shard_map/all_to_all | solution.py:52
  407.9 4.9 %copy-start.3 = (f32[64,3584]{0,1:T(8,128)S(1)}, f32[64,3584]{0,1:T(8,128)}, u32[]{:S(2)}) copy-start(f32[64,3584]{0,1:T(8,128)} %copy.127) | copy-start | bytes 2752516
  414.3 6.7 %copy-start.1 = (bf16[256,3584]{1,0:T(8,128)(2,1)S(1)}, bf16[256,3584]{1,0:T(8,128)(2,1)}, u32[]{:S(2)}) copy-start(bf16[256,3584]{1,0:T(8,128)(2,1)} %param.11) | copy-start | bytes 5505028
Sparse Core Ops, SparseCore 0:
  20.4 49.4 all-gather.5
  71.7 21.7 all-gather.7
  96.2 81.5 all-gather.9
where the time goes:
time: 430 us; the launch traced here: 429 us
  waiting for transfers between devices  241 us (56%)
  blocking collectives  71.3 us (17%)
  local copies, waits for them, and re-layouts  38.2 us (9%)
  starting transfers between devices  31.5 us (7%)
  matrix products  18.6 us (4%)
  between operations  17.9 us (4%)
  other arithmetic  10.5 us (2%)
    all_gather x2, waiting for transfers between devices, all_blocks(): parts = lax.all_gather(parts, axes[k], axis=0, tiled=True)  69.5 us
    all_gather x1, waiting for transfers between devices, per_device(): lax.all_gather(w_out, POP, axis=1, tiled=True)  65.1 us
    all_gather x1, blocking collectives, side_by_side(): result, at, done = (lax.all_gather(both, axis, axis=dim, tiled=True), 0, [])  51.8 us
    all_to_all x1, waiting for transfers between devices, per_device(): lax.all_to_all(query_left_factors, POP, split_axis=1, concat_axis=0, tile...  44 us
    all_to_all x1, waiting for transfers between devices, per_device(): lax.all_to_all(o_right, POP, split_axis=2, concat_axis=0, tiled=True)  38.7 us
    all_to_all x1, waiting for transfers between devices, summed_on_arrival(): lax.all_to_all(cut_along(shard, dim, devices), axis, 0, 0, tiled=True)  22.5 us
    all_to_all x2, starting transfers between devices, copy_for_each(): return lax.all_to_all(copies, axis, split_axis=0, concat_axis=0, tiled=True)  14 us
    all_gather x1, blocking collectives, all_blocks(): parts = lax.all_gather(parts, axes[k], axis=0, tiled=True)  13 us
  transfers between devices with their start and end apart: 8, of which 7 were waited for; matrix products, arithmetic and copies ran while one was open for 9% of the time, Pallas kernels for 0%

commit v1 on v0

--- a/solution.py
+++ b/solution.py
@@ -146,7 +146,7 @@
     part = jnp.einsum(
         "mtf,fe->mte",
         mixed,
-        lax.all_gather(w_out, POP, axis=1, tiled=True),
+        jnp.concatenate(lax.all_gather(w_out, POP), axis=1),
         preferred_element_type=jnp.float32,
     )
     term = part + factor * jnp.einsum(

time: 430 us -> 436 us (1.014)
  local copies, waits for them, and re-layouts: 38.2 us -> 45.9 us
    unnamed x35 -> x36, local copies, waits for them, and re-layouts: 12 us -> 16.1 us
where the time goes in v1:
time: 436 us; the launch traced here: 435 us
  waiting for transfers between devices  241 us (55%)
  blocking collectives  71.3 us (16%)
  local copies, waits for them, and re-layouts  45.9 us (11%)
  starting transfers between devices  31.9 us (7%)
  between operations  18 us (4%)
  matrix products  16 us (4%)
  other arithmetic  10.5 us (2%)
    all_gather x2, waiting for transfers between devices, all_blocks(): parts = lax.all_gather(parts, axes[k], axis=0, tiled=True)  69.5 us
    all_gather x1, waiting for transfers between devices, per_device(): lax.all_gather(w_out, POP)  65.4 us
    all_gather x1, blocking collectives, side_by_side(): result, at, done = (lax.all_gather(both, axis, axis=dim, tiled=True), 0, [])  51.8 us
    all_to_all x1, waiting for transfers between devices, per_device(): lax.all_to_all(query_left_factors, POP, split_axis=1, concat_axis=0, tile...  44 us
    all_to_all x1, waiting for transfers between devices, per_device(): lax.all_to_all(o_right, POP, split_axis=2, concat_axis=0, tiled=True)  38.7 us
    all_to_all x1, waiting for transfers between devices, summed_on_arrival(): lax.all_to_all(cut_along(shard, dim, devices), axis, 0, 0, tiled=True)  22.5 us
    unnamed x36, local copies, waits for them, and re-layouts  16.1 us
    all_to_all x2, starting transfers between devices, copy_for_each(): return lax.all_to_all(copies, axis, split_axis=0, concat_axis=0, tiled=True)  14.4 us
  transfers between devices with their start and end apart: 8, of which 7 were waited for; matrix products, arithmetic and copies ran while one was open for 9% of the time, Pallas kernels for 0%

profile of v1, /device:TPU:1, one launch (start us, length us, event | category | flops | bytes accessed | tf_op | source)
XLA Modules:
  0.0 434.6 jit_solution(13605954745094671707)
XLA Ops:
  7.2 13.0 %all-gather = bf16[224,896]{1,0:T(8,128)(2,1)} all-gather(bf16[56,896]{1,0:T(8,128)(2,1)} %param.13), channel_id=2, replica_groups=mesh['pop_0'=4,'pop_1'=8,'pop_2'=2,'mp'=4] {'pop_0'}, dimensions={0}, use_global_device_ids=true | all-gather | bytes 501760 | tf_op jit(solution)/shard_map/all_gather | solution.py:28
  20.3 49.6 %all-gather.7.cloned.1.call-done = bf16[32,56,896]{2,1,0:T(8,128)(2,1)} async-done(((bf16[4,56,896]{2,1,0:T(8,128)(2,1)}), bf16[32,56,896]{2,1,0:T(8,128)(2,1)}) %all-gather.7.cloned.1.call-update) | async-done | bytes 3211280 | tf_op jit(solution)/shard_map/all_gather | solution.py:28
  73.6 19.9 %all-gather.9.cloned.1.call-done = bf16[64,56,896]{2,1,0:T(8,128)(2,1)} async-done(((bf16[32,56,896]{2,1,0:T(8,128)(2,1)}), bf16[64,56,896]{2,1,0:T(8,128)(2,1)}) %all-gather.9.cloned.1.call-update) | async-done | bytes 6422544 | tf_op jit(solution)/shard_map/all_gather | solution.py:28
  93.5 3.3 copy.119
  96.9 2.1 fusion.29
  99.1 2.1 fusion.3
  110.0 2.6 convolution_convert_fusion
  112.8 65.4 %all-gather.11.cloned.1.call-done = bf16[57344,56]{0,1:T(8,128)(2,1)} async-done(((bf16[896,56]{0,1:T(8,128)(2,1)}), bf16[57344,56]{0,1:T(8,128)(2,1)}) %all-gather.11.cloned.1.call-update) | async-done | bytes 6422544 | tf_op jit(solution)/shard_map/all_gather | solution.py:149
  178.1 4.0 copy.148
  182.2 3.7 copy.126
  185.9 2.4 fusion.30
  188.2 3.1 fusion.1
  191.3 3.3 reshape.296
  194.7 1.5 copy.152
  196.2 4.0 all-to-all-start.1
  200.7 22.5 %all-to-all-done.1 = bf16[4,1,256,896]{3,2,1,0:T(8,128)(2,1)S(1)} async-done(((bf16[4,1,256,896]{3,2,1,0:T(8,128)(2,1)}), bf16[4,1,256,896]{3,2,1,0:T(8,128)(2,1)S(1)}, u32[]{:S(2)}, u32[]{:S(2)}) %all-to-all-start.1) | async-done | bytes 1835040 | tf_op jit(solution)/shard_map/all_to_all | solution.py:46
  225.0 6.5 %all_to_all.47 = f32[4,1,1]{2,1,0:T(1,128)S(1)} all-to-all(f32[4,1,1]{2,1,0:T(1,128)S(1)} %broadcast_in_dim.34), channel_id=1, replica_groups=mesh['pop_0'=4,'pop_1'=8,'pop_2'=2,'mp'=4] {'mp'}, dimensions={0} | all-to-all | bytes 32 | tf_op jit(solution)/shard_map/all_to_all | solution.py:52
  233.4 8.1 %all-to-all-start.3 = ((f32[64,1,1]{2,1,0:T(1,128)}), f32[64,1,1]{2,1,0:T(1,128)S(1)}, u32[]{:S(2)}, u32[]{:S(2)}) async-start(f32[64,1,1]{2,1,0:T(1,128)} %broadcast_in_dim.35), calls=%async_computation.3 | async-start | bytes 65536 | tf_op jit(solution)/shard_map/all_to_all | solution.py:52
  241.5 51.8 %all-gather.2 = bf16[64,1,7168]{2,1,0:T(2,128)(2,1)S(1)} all-gather(bf16[1,1,7168]{2,1,0:T(2,128)(2,1)S(1)} %maximum_bitcast_fusion.2), channel_id=1, replica_groups=mesh['pop_0'=4,'pop_1'=8,'pop_2'=2,'mp'=4] {'pop_0','pop_1','pop_2'}, dimensions={0}, use_global_device_ids=true | all-gather | bytes 931840 | tf_op jit(solution)/shard_map/all_gather | solution.py:66
  293.3 3.2 copy.135
  297.8 7.3 %all-to-all-start.5 = ((bf16[1,4,3584]{1,0,2:T(2,128)(2,1)}), bf16[1,4,3584]{1,0,2:T(2,128)(2,1)S(1)}, u32[]{:S(2)}, u32[]{:S(2)}) async-start(bf16[1,4,3584]{1,0,2:T(2,128)(2,1)} %copy.135), calls=%async_computation.5 | async-start | bytes 3670016 | tf_op jit(solution)/shard_map/all_to_all | solution.py:167
  305.0 2.0 slice_convert_fusion
  307.1 3.2 copy.117
  311.7 38.7 %all-to-all-done.5 = bf16[1,4,3584]{1,0,2:T(2,128)(2,1)S(1)} async-done(((bf16[1,4,3584]{1,0,2:T(2,128)(2,1)}), bf16[1,4,3584]{1,0,2:T(2,128)(2,1)S(1)}, u32[]{:S(2)}, u32[]{:S(2)}) %all-to-all-start.5) | async-done | bytes 28704 | tf_op jit(solution)/shard_map/all_to_all | solution.py:167
  350.4 6.2 %all-to-all-start = ((bf16[1,3584,4]{2,0,1:T(2,128)(2,1)}), bf16[1,3584,4]{2,0,1:T(2,128)(2,1)}, u32[]{:S(2)}, u32[]{:S(2)}) async-start(bf16[1,3584,4]{2,0,1:T(2,128)(2,1)} %copy.117), calls=%async_computation | async-start | bytes 3670016 | tf_op jit(solution)/shard_map/all_to_all | solution.py:166
  357.9 44.0 %all-to-all-done = bf16[1,3584,4]{2,0,1:T(2,128)(2,1)} async-done(((bf16[1,3584,4]{2,0,1:T(2,128)(2,1)}), bf16[1,3584,4]{2,0,1:T(2,128)(2,1)}, u32[]{:S(2)}, u32[]{:S(2)}) %all-to-all-start) | async-done | bytes 28704 | tf_op jit(solution)/shard_map/all_to_all | solution.py:166
  402.5 6.2 %all-to-all-start.4 = ((f32[64,1,1]{2,1,0:T(1,128)}), f32[64,1,1]{2,1,0:T(1,128)S(1)}, u32[]{:S(2)}, u32[]{:S(2)}) async-start(f32[64,1,1]{2,1,0:T(1,128)} %broadcast_in_dim.36), calls=%async_computation.4 | async-start | bytes 65536 | tf_op jit(solution)/shard_map/all_to_all | solution.py:52
  408.8 1.8 copy.133
  411.9 1.8 copy.136
  413.9 3.7 copy.118
  418.6 1.6 multiply_bitcast_fusion
  420.2 2.8 copy.134
  (73 shorter events, 25.1 us)
Async XLA Ops:
  7.2 64.2 %copy-start = (bf16[256,3584]{1,0:T(8,128)(2,1)S(1)}, bf16[256,3584]{1,0:T(8,128)(2,1)}, u32[]{:S(2)}) copy-start(bf16[256,3584]{1,0:T(8,128)(2,1)} %param.11) | copy-start | bytes 5505028
  7.2 62.7 %all-gather.7.cloned.1.call-start = ((), (), s32[]{:S(2)}) async-start(), calls=%async_computation.6 | async-start | bytes 3612672 | tf_op jit(solution)/shard_map/all_gather | solution.py:28
  20.2 51.2 %copy-start.4 = (bf16[3584,128]{1,0:T(8,128)(2,1)S(1)}, bf16[3584,128]{1,0:T(8,128)(2,1)}, u32[]{:S(2)}) copy-start(bf16[3584,128]{1,0:T(8,128)(2,1)} %param.14) | copy-start | bytes 2752516
  20.3 73.3 %all-gather.9.cloned.1.call-start = ((), (), s32[]{:S(2)}) async-start(), calls=%async_computation.7 | async-start | bytes 9633792 | tf_op jit(solution)/shard_map/all_gather | solution.py:28
  69.9 108.2 %all-gather.11.cloned.1.call-start = ((), (), s32[]{:S(2)}) async-start(), calls=%async_computation.8 | async-start | bytes 6522880 | tf_op jit(solution)/shard_map/all_gather | solution.py:149
  96.9 2.2 copy-start.9
  96.9 2.2 copy-start.11
  106.1 1.4 copy-start.6
  106.1 1.4 copy-start.7
  108.1 1.3 copy-start.2
  108.2 1.8 copy-start.13
  110.0 2.6 copy-start.12
  185.9 2.4 copy-start.8
  196.2 27.1 %all-to-all-start.1 = ((bf16[4,1,256,896]{3,2,1,0:T(8,128)(2,1)}), bf16[4,1,256,896]{3,2,1,0:T(8,128)(2,1)S(1)}, u32[]{:S(2)}, u32[]{:S(2)}) async-start(bf16[4,1,256,896]{3,2,1,0:T(8,128)(2,1)} %bitcast.105), calls=%async_computation.1 | async-start | bytes 3670016 | tf_op jit(solution)/shard_map/all_to_all | solution.py:46
  200.2 23.3 %copy-start.5 = (bf16[256,896]{1,0:T(8,128)(2,1)S(1)}, bf16[256,896]{1,0:T(8,128)(2,1)}, u32[]{:S(2)}) copy-start(bf16[256,896]{1,0:T(8,128)(2,1)} %param.12) | copy-start | bytes 1376260
  233.4 64.4 %all-to-all-start.3 = ((f32[64,1,1]{2,1,0:T(1,128)}), f32[64,1,1]{2,1,0:T(1,128)S(1)}, u32[]{:S(2)}, u32[]{:S(2)}) async-start(f32[64,1,1]{2,1,0:T(1,128)} %broadcast_in_dim.35), calls=%async_computation.3 | async-start | bytes 65536 | tf_op jit(solution)/shard_map/all_to_all | solution.py:52
  297.8 52.7 %all-to-all-start.5 = ((bf16[1,4,3584]{1,0,2:T(2,128)(2,1)}), bf16[1,4,3584]{1,0,2:T(2,128)(2,1)S(1)}, u32[]{:S(2)}, u32[]{:S(2)}) async-start(bf16[1,4,3584]{1,0,2:T(2,128)(2,1)} %copy.135), calls=%async_computation.5 | async-start | bytes 3670016 | tf_op jit(solution)/shard_map/all_to_all | solution.py:167
  305.0 2.1 copy-start.10
  350.4 51.5 %all-to-all-start = ((bf16[1,3584,4]{2,0,1:T(2,128)(2,1)}), bf16[1,3584,4]{2,0,1:T(2,128)(2,1)}, u32[]{:S(2)}, u32[]{:S(2)}) async-start(bf16[1,3584,4]{2,0,1:T(2,128)(2,1)} %copy.117), calls=%async_computation | async-start | bytes 3670016 | tf_op jit(solution)/shard_map/all_to_all | solution.py:166
  402.5 15.5 %all-to-all-start.4 = ((f32[64,1,1]{2,1,0:T(1,128)}), f32[64,1,1]{2,1,0:T(1,128)S(1)}, u32[]{:S(2)}, u32[]{:S(2)}) async-start(f32[64,1,1]{2,1,0:T(1,128)} %broadcast_in_dim.36), calls=%async_computation.4 | async-start | bytes 65536 | tf_op jit(solution)/shard_map/all_to_all | solution.py:52
  413.7 4.9 %copy-start.3 = (f32[64,3584]{0,1:T(8,128)S(1)}, f32[64,3584]{0,1:T(8,128)}, u32[]{:S(2)}) copy-start(f32[64,3584]{0,1:T(8,128)} %copy.133) | copy-start | bytes 2752516
  420.2 6.7 %copy-start.1 = (bf16[256,3584]{1,0:T(8,128)(2,1)S(1)}, bf16[256,3584]{1,0:T(8,128)(2,1)}, u32[]{:S(2)}) copy-start(bf16[256,3584]{1,0:T(8,128)(2,1)} %param.11) | copy-start | bytes 5505028
Sparse Core Ops, SparseCore 0:
  20.4 49.4 all-gather.6
  71.7 21.7 all-gather.8
  96.2 81.8 all-gather.10
